TPU v7x, 32 devices: a whole 2x2x4 slice. The times are simulated.
32 devices in a mesh: samp: 8 (over y, x, core), par: 4 (over z).
Axes of the slice: x: 2, y: 2, z: 4, core: 2. Of those that a mesh axis runs over, the one named last changes fastest.
Arguments:
- log_derivs: bfloat16 [512, 262144], P('samp', 'par')
- energies: float32 [512, 8], P('samp'), may hold values from -6 to 6
- nys_rows: int32 [8, 8], P('samp'), may hold values from 0 to 63, as said below
Outputs:
- update: float32 [262144, 8], P('par')
- solution: float32 [512, 8], P('samp')
Inputs may be any that keep to these rules, and one draw needn't show every extreme that they name: `nys_rows`: each row holds 8 different local sample numbers of that group.
All inputs are finite; a program needn't handle non-finite values.
Results may differ from a plain program's by a relative error of at most 0.014.
Values may be sent and summed in bfloat16 or wider, within the bound.
A program may use at most 128 MiB of HBM per device.

v0:
```python
import math
import jax
import jax.numpy as jnp
from jax import lax
from jax.sharding import PartitionSpec as P

ITERS = 2
damping = 0.5


def factor_solve(factor, right):
    middle = lax.linalg.triangular_solve(factor, right, left_side=True, lower=True)
    return lax.linalg.triangular_solve(factor, middle, left_side=True, lower=True, transpose_a=True)


def small_solve(matrix, right):
    return factor_solve(jnp.linalg.cholesky(matrix), right)


def hdot(left, right):
    return jnp.dot(left, right, precision=lax.Precision.HIGHEST)


def gram_body(log_derivs, energies, nys_rows):
    samp_rows = log_derivs.shape[0]
    groups = lax.axis_size("samp")
    total_rows = samp_rows * groups
    total_cols = log_derivs.shape[1] * lax.axis_size("par")
    slab = lax.all_to_all(log_derivs, "samp", split_axis=1, concat_axis=0, tiled=True)
    widened = slab.astype(jnp.float32)
    col_mean = jnp.sum(widened, axis=0) / total_rows
    centered = ((widened - col_mean) * (1.0 / math.sqrt(total_cols))).astype(jnp.bfloat16)
    gram = lax.psum(
        jnp.einsum("rc,kc->rk", centered, centered, preferred_element_type=jnp.float32),
        ("samp", "par"),
    )
    all_energies = lax.all_gather(energies, "samp", axis=0, tiled=True)
    all_picks = lax.all_gather(nys_rows, "samp", axis=0, tiled=True)
    selected = (jnp.arange(groups, dtype=jnp.int32)[:, None] * samp_rows + all_picks).reshape(-1)
    sketch = jnp.take(gram, selected, axis=1)
    core_block = jnp.take(sketch, selected, axis=0)
    factor = jnp.linalg.cholesky(damping * core_block + hdot(sketch.T, sketch))

    def precondition(residual):
        coeffs = factor_solve(factor, hdot(sketch.T, residual))
        result = (residual - hdot(sketch, coeffs)) / damping
        return (result, hdot(result.T, residual))

    solution = jnp.zeros(all_energies.shape, jnp.float32)
    residual = all_energies
    precond_res, inner_prev = precondition(residual)
    direction = precond_res
    for iteration in range(ITERS):
        rounded = direction.astype(jnp.bfloat16).astype(jnp.float32)
        image_k = hdot(gram, rounded) + damping * direction
        curvature = hdot(direction.T, image_k)
        alpha_k = small_solve(curvature, inner_prev)
        solution = solution + hdot(direction, alpha_k)
        if iteration + 1 < ITERS:
            residual = residual - hdot(image_k, alpha_k)
            precond_res, inner_next = precondition(residual)
            beta_k = small_solve(inner_prev, inner_next)
            direction = precond_res + hdot(direction, beta_k)
            inner_prev = inner_next
    rounded_sol = solution.astype(jnp.bfloat16)
    local_update = jnp.einsum(
        "rc,rv->cv", centered, rounded_sol, preferred_element_type=jnp.float32
    )
    update = lax.all_gather(local_update.astype(jnp.bfloat16), "samp", axis=0, tiled=True).astype(
        local_update.dtype
    )
    start = lax.axis_index("samp") * samp_rows
    return (update, lax.dynamic_slice_in_dim(solution, start, samp_rows, 0))


def body(log_derivs, energies, nys_rows):
    update, solution = gram_body(log_derivs, energies, nys_rows)
    return (update, solution)


def solution(mesh):
    return jax.shard_map(
        body,
        mesh=mesh,
        in_specs=(P("samp", "par"), P("samp", None), P("samp", None)),
        out_specs=(P("par", None), P("samp", None)),
        check_vma=False,
    )
```

profile of v0, /device:TPU:0, one launch (start us, length us, event | category | flops | bytes accessed | tf_op | source)
XLA Modules:
  0.0 351.4 jit_solution(1456690422608163181)
XLA Ops:
  7.2 7.6 %copy.62 = bf16[8,8,8,8192]{3,2,0,1:T(8,128)(2,1)} copy(bf16[8,8,8,8192]{3,2,1,0:T(8,128)(2,1)} %bitcast.122) | data formatting | bytes 16777216 | tf_op jit(solution)/shard_map/all_to_all | solution.py:29
  14.8 5.3 %all-to-all-start = ((bf16[64,8,8192]{2,0,1:T(8,128)(2,1)}), bf16[64,8,8192]{2,0,1:T(8,128)(2,1)}, u32[]{:S(2)}, u32[]{:S(2)}) async-start(bf16[64,8,8192]{2,0,1:T(8,128)(2,1)} %bitcast.121), calls=%async_computation | async-start | bytes 16777216 | tf_op jit(solution)/shard_map/all_to_all | solution.py:29
  20.1 97.4 %all-gather.1 = s32[8,1,8]{2,1,0:T(1,128)S(1)} all-gather(s32[1,1,8]{2,1,0:T(1,128)S(1)} %bitcast.126), channel_id=1, replica_groups=mesh['samp'=8,'par'=4] {'samp'}, dimensions={0}, use_global_device_ids=true | all-gather | bytes 288 | tf_op jit(solution)/shard_map/all_gather | solution.py:38
  117.7 8.3 %all-gather = f32[8,64,8]{1,2,0:T(8,128)S(1)} all-gather(f32[1,64,8]{1,2,0:T(8,128)S(1)} %bitcast.125), channel_id=1, replica_groups=mesh['samp'=8,'par'=4] {'samp'}, dimensions={0}, use_global_device_ids=true | all-gather | bytes 18432 | tf_op jit(solution)/shard_map/all_gather | solution.py:37
  126.1 5.5 %convert_reduce_fusion = f32[8192]{0:T(1024)S(1)} fusion(bf16[64,8,8192]{2,0,1:T(8,128)(2,1)} %all-to-all-done), kind=kLoop, calls=%fused_computation.8 | loop fusion | flops 8380416 | bytes 8421376 | tf_op jit(solution)/shard_map/reduce_sum | solution.py:31
  131.6 8.9 %multiply_convert_fusion = bf16[64,8,8192]{2,0,1:T(8,128)(2,1)} fusion(bf16[64,8,8192]{2,0,1:T(8,128)(2,1)} %all-to-all-done, f32[8192]{0:T(1024)S(1)} %broadcast_multiply_fusion), kind=kLoop, calls=%fused_computation.5 | loop fusion | flops 16777216 | bytes 16809984 | tf_op jit(solution)/shard_map/convert.2
  140.5 11.3 %fusion.73 = f32[512,512]{1,0:T(8,128)} fusion(bf16[512,8192]{1,0:T(8,128)(2,1)} %bitcast.123), kind=kOutput, calls=%fused_computation.118 | convolution fusion | flops 4294967296 | bytes 9437184 | tf_op jit(solution)/shard_map/rc,kc->rk/dot_general | solution.py:34
  151.8 0.2 all-gather.4.cloned.1.call-start
  152.0 8.9 %fusion.1 = bf16[512,8192]{1,0:T(8,128)(2,1)} fusion(bf16[64,8,8192]{2,0,1:T(8,128)(2,1)} %all-to-all-done, f32[8192]{0:T(1024)S(1)} %broadcast_multiply_fusion), kind=kLoop, calls=%fused_computation.4 | loop fusion | flops 16777216 | bytes 16809984 | tf_op jit(solution)/shard_map/convert_element_type | solution.py:32
  160.9 122.7 %all-reduce.2.cloned.1.call-done = f32[512,512]{1,0:T(8,128)} async-done(((f32[512,512]{1,0:T(8,128)}), f32[512,512]{1,0:T(8,128)}) %all-reduce.2.cloned.1.call-update) | async-done | bytes 1048592 | tf_op jit(solution)/shard_map/psum | solution.py:33
  283.6 1.6 copy.48
  285.2 0.7 gather_fusion
  286.1 0.6 gather_fusion.1
  286.7 0.3 convolution_add_fusion
  287.2 5.8 %cholesky.33 = f32[64,64]{1,0:T(8,128)S(1)} custom-call(f32[64,64]{1,0:T(8,128)S(1)} %fusion.29), custom_call_target="Cholesky" | custom-call | tf_op jit(solution)/shard_map/jit(cholesky)/cholesky | solution.py:42
  293.1 0.6 compare_reduce_fusion.3
  293.7 0.7 fusion.20
  294.4 4.9 %custom-call.24 = f32[1,64,64]{1,2,0:T(8,128)S(1)} custom-call(f32[1,64,64]{2,1,0:T(8,128)S(1)} %fusion.20), custom_call_target="InvertDiagBlocksLowerTriangular" | custom-call | tf_op jit(solution)/shard_map/triangular_solve/custom-call.3 | solution.py:13
  299.3 0.3 fusion.7
  299.5 0.2 fusion.25
  299.9 0.3 convolution_subtract_fusion.2
  300.4 1.8 convolution_add_fusion.4
  302.4 0.7 cholesky.94
  303.2 0.6 compare_reduce_fusion.2
  303.8 0.6 fusion.44
  304.5 0.6 custom-call.26
  305.1 0.2 fusion.55
  305.4 0.2 convolution_subtract_fusion.1
  305.6 0.2 fusion.31
  305.9 0.7 cholesky.105
  306.6 0.6 compare_reduce_fusion.1
  307.3 0.6 fusion.45
  307.9 0.6 custom-call.30
  308.5 0.3 fusion.4
  309.1 0.3 fusion.2
  309.6 0.2 fusion.51
  309.9 0.2 convolution_add_fusion.3
  310.1 0.6 convolution_add_fusion.2
  310.9 0.7 cholesky.116
  311.7 0.6 compare_reduce_fusion
  312.4 0.6 fusion.46
  313.0 0.6 custom-call.32
  313.6 0.2 fusion.47
  314.0 0.2 convolution_add_fusion.1
  314.2 5.2 %convolution_convert_fusion = bf16[8192,8]{0,1:T(8,128)(2,1)} fusion(bf16[512,8192]{1,0:T(8,128)(2,1)} %fusion.1, f32[512,8]{0,1:T(8,128)S(1)} %convolution_add_fusion.1), kind=kOutput, calls=%fused_computation.6 | convolution fusion | flops 67178496 | bytes 8536064 | tf_op jit(solution)/shard_map/rc,rv->cv/dot_general | solution.py:66
  319.5 0.7 constant_dynamic-slice_fusion
  320.1 21.8 %all-gather.4.cloned.1.call-done = bf16[65536,8]{0,1:T(8,128)(2,1)} async-done(((bf16[8192,8]{0,1:T(8,128)(2,1)}), bf16[65536,8]{0,1:T(8,128)(2,1)}) %all-gather.4.cloned.1.call-update) | async-done | bytes 1048592 | tf_op jit(solution)/shard_map/all_gather | solution.py:69
  341.9 2.7 convert_element_type.49
  (44 shorter events, 2.7 us)
Async XLA Ops:
  14.8 5.4 %copy-start.2 = (s32[1,8]{1,0:T(1,128)S(1)}, s32[1,8]{1,0:T(1,128)}, u32[]{:S(2)}) copy-start(s32[1,8]{1,0:T(1,128)} %param.14) | copy-start | bytes 100
  14.8 103.0 %copy-start.1 = (f32[64,8]{0,1:T(8,128)S(1)}, f32[64,8]{0,1:T(8,128)}, u32[]{:S(2)}) copy-start(f32[64,8]{0,1:T(8,128)} %param.13) | copy-start | bytes 6148
  14.8 111.4 %all-to-all-start = ((bf16[64,8,8192]{2,0,1:T(8,128)(2,1)}), bf16[64,8,8192]{2,0,1:T(8,128)(2,1)}, u32[]{:S(2)}, u32[]{:S(2)}) async-start(bf16[64,8,8192]{2,0,1:T(8,128)(2,1)} %bitcast.121), calls=%async_computation | async-start | bytes 16777216 | tf_op jit(solution)/shard_map/all_to_all | solution.py:29
  20.1 263.5 %all-reduce.2.cloned.1.call-start = ((), (), s32[]{:S(2)}) async-start(), calls=%async_computation.1 | async-start | bytes 2097152 | tf_op jit(solution)/shard_map/psum | solution.py:33
  151.8 190.1 %all-gather.4.cloned.1.call-start = ((), (), s32[]{:S(2)}) async-start(), calls=%async_computation.2 | async-start | bytes 1179648 | tf_op jit(solution)/shard_map/all_gather | solution.py:69
  283.6 26.5 %copy-start = (f32[512,512]{1,0:T(8,128)S(1)}, f32[512,512]{1,0:T(8,128)}, u32[]{:S(2)}) copy-start(f32[512,512]{1,0:T(8,128)} %all-reduce.2.cloned.1.call-done) | copy-start | bytes 3145732
Sparse Core Ops, SparseCore 0:
  151.9 131.6 all-reduce.1
  319.6 22.3 all-gather.3
where the time goes:
time: 352 us; the launch traced here: 351 us
  waiting for transfers between devices  145 us (41%)
  blocking collectives  106 us (30%)
  other arithmetic  46.2 us (13%)
  matrix products  23.4 us (7%)
  between operations  14.2 us (4%)
  local copies, waits for them, and re-layouts  11.8 us (3%)
  starting transfers between devices  5.59 us (2%)
    psum x1, waiting for transfers between devices, gram_body(): lax.psum(jnp.einsum('rc,kc->rk', centered, centered, preferred_element_ty...  123 us
    all_gather x1, blocking collectives, gram_body(): all_picks = lax.all_gather(nys_rows, 'samp', axis=0, tiled=True)  97.4 us
    all_gather x1, waiting for transfers between devices, gram_body(): lax.all_gather(local_update.astype(jnp.bfloat16), 'samp', axis=0, tiled=T...  21.8 us
    dot_general x1, matrix products, gram_body(): jnp.einsum('rc,kc->rk', centered, centered, preferred_element_type=jnp.fl...  11.3 us
    another operation x8, other arithmetic, factor_solve(): lax.linalg.triangular_solve(factor, middle, left_side=True, lower=True, t...  9.37 us
    another operation x1, other arithmetic  8.89 us
    convert_element_type x1, other arithmetic, gram_body(): ((widened - col_mean) * (1.0 / math.sqrt(total_cols))).astype(jnp.bfloat16)  8.89 us
    all_gather x1, blocking collectives, gram_body(): all_energies = lax.all_gather(energies, 'samp', axis=0, tiled=True)  8.27 us
  transfers between devices with their start and end apart: 3, of which 2 were waited for; matrix products, arithmetic and copies ran while one was open for 3% of the time, Pallas kernels for 0%

commit v1 on v0

--- a/solution.py
+++ b/solution.py
@@ -31,8 +31,10 @@
     col_mean = jnp.sum(widened, axis=0) / total_rows
     centered = ((widened - col_mean) * (1.0 / math.sqrt(total_cols))).astype(jnp.bfloat16)
     gram = lax.psum(
-        jnp.einsum("rc,kc->rk", centered, centered, preferred_element_type=jnp.float32),
-        ("samp", "par"),
+        lax.psum(
+            jnp.einsum("rc,kc->rk", centered, centered, preferred_element_type=jnp.float32), "par"
+        ),
+        "samp",
     )
     all_energies = lax.all_gather(energies, "samp", axis=0, tiled=True)
     all_picks = lax.all_gather(nys_rows, "samp", axis=0, tiled=True)

time: 352 us -> 319 us (0.906)
  waiting for transfers between devices: 145 us -> 106 us
  blocking collectives: 106 us -> 116 us
  starting transfers between devices: 5.59 us -> 0.3 us
    all_to_all x0 -> x1, blocking collectives: none -> 99.2 us  [gram_body(): lax.all_to_all(log_derivs, 'samp', split_axis=1, concat_axis=0, tiled=True)]
    all_gather x1, blocking collectives: 97.4 us -> 7.85 us  [gram_body(): all_picks = lax.all_gather(nys_rows, 'samp', axis=0, tiled=True)]
    psum x1, waiting for transfers between devices: 123 us -> 34.2 us  [gram_body(): lax.psum(jnp.einsum('rc,kc->rk', centered, centered, preferred_element_ty...]
    psum x0 -> x1, waiting for transfers between devices: none -> 50 us  [gram_body(): lax.psum(lax.psum(jnp.einsum('rc,kc->rk', centered, centered, preferred_e...]
    all_to_all x1 -> x0, starting transfers between devices: 5.33 us -> none  [gram_body(): lax.all_to_all(log_derivs, 'samp', split_axis=1, concat_axis=0, tiled=True)]
  transfers between devices with their start and end apart: 3 -> 3, of which waited for: 2 -> 3; matrix products, arithmetic and copies ran while one was open for 3% -> 3% of each run, Pallas kernels for 0% -> 0%
where the time goes in v1:
time: 319 us; the launch traced here: 318 us
  blocking collectives  116 us (36%)
  waiting for transfers between devices  106 us (33%)
  other arithmetic  42.9 us (13%)
  matrix products  23.5 us (7%)
  local copies, waits for them, and re-layouts  15.1 us (5%)
  between operations  13.9 us (4%)
    all_to_all x1, blocking collectives, gram_body(): lax.all_to_all(log_derivs, 'samp', split_axis=1, concat_axis=0, tiled=True)  99.2 us
    psum x1, waiting for transfers between devices, gram_body(): lax.psum(lax.psum(jnp.einsum('rc,kc->rk', centered, centered, preferred_e...  50 us
    psum x1, waiting for transfers between devices, gram_body(): lax.psum(jnp.einsum('rc,kc->rk', centered, centered, preferred_element_ty...  34.2 us
    all_gather x1, waiting for transfers between devices, gram_body(): lax.all_gather(local_update.astype(jnp.bfloat16), 'samp', axis=0, tiled=T...  22.1 us
    dot_general x1, matrix products, gram_body(): jnp.einsum('rc,kc->rk', centered, centered, preferred_element_type=jnp.fl...  11.3 us
    another operation x8, other arithmetic, factor_solve(): lax.linalg.triangular_solve(factor, middle, left_side=True, lower=True, t...  9.37 us
    all_gather x1, blocking collectives, gram_body(): all_energies = lax.all_gather(energies, 'samp', axis=0, tiled=True)  9.06 us
    another operation x1, other arithmetic  8.89 us
  transfers between devices with their start and end apart: 3, of which 3 were waited for; matrix products, arithmetic and copies ran while one was open for 3% of the time, Pallas kernels for 0%

profile of v1, /device:TPU:0, one launch (start us, length us, event | category | flops | bytes accessed | tf_op | source)
XLA Modules:
  0.0 318.0 jit_solution(13652448125382300747)
XLA Ops:
  7.2 7.6 %copy.62 = bf16[8,8,8,8192]{3,2,0,1:T(8,128)(2,1)} copy(bf16[8,8,8,8192]{3,2,1,0:T(8,128)(2,1)} %bitcast.122) | data formatting | bytes 16777216 | tf_op jit(solution)/shard_map/all_to_all | solution.py:29
  14.8 99.2 %all_to_all.13 = bf16[64,8,8192]{2,0,1:T(8,128)(2,1)S(1)} all-to-all(bf16[64,8,8192]{2,0,1:T(8,128)(2,1)} %bitcast.121), channel_id=1, replica_groups=mesh['samp'=8,'par'=4] {'samp'}, dimensions={1} | all-to-all | bytes 16777216 | tf_op jit(solution)/shard_map/all_to_all | solution.py:29
  114.0 3.2 %copy-done = bf16[64,8,8192]{2,0,1:T(8,128)(2,1)} copy-done((bf16[64,8,8192]{2,0,1:T(8,128)(2,1)}, bf16[64,8,8192]{2,0,1:T(8,128)(2,1)S(1)}, u32[]{:S(2)}) %copy-start) | copy-done | bytes 8388632
  117.2 2.1 convert_reduce_fusion
  119.4 8.9 %multiply_convert_fusion = bf16[64,8,8192]{2,0,1:T(8,128)(2,1)} fusion(bf16[64,8,8192]{2,0,1:T(8,128)(2,1)} %copy-done, f32[8192]{0:T(1024)S(1)} %broadcast_multiply_fusion), kind=kLoop, calls=%fused_computation.5 | loop fusion | flops 16777216 | bytes 16809984 | tf_op jit(solution)/shard_map/convert.2
  128.3 11.3 %fusion.73 = f32[512,512]{1,0:T(8,128)} fusion(bf16[512,8192]{1,0:T(8,128)(2,1)} %bitcast.123), kind=kOutput, calls=%fused_computation.118 | convolution fusion | flops 4294967296 | bytes 9437184 | tf_op jit(solution)/shard_map/rc,kc->rk/dot_general | solution.py:35
  139.6 7.8 %all-gather.1 = s32[8,1,8]{2,1,0:T(1,128)S(1)} all-gather(s32[1,1,8]{2,1,0:T(1,128)S(1)} %bitcast.126), channel_id=1, replica_groups=mesh['samp'=8,'par'=4] {'samp'}, dimensions={0}, use_global_device_ids=true | all-gather | bytes 288 | tf_op jit(solution)/shard_map/all_gather | solution.py:40
  147.7 9.1 %all-gather = f32[8,64,8]{1,2,0:T(8,128)S(1)} all-gather(f32[1,64,8]{1,2,0:T(8,128)S(1)} %bitcast.125), channel_id=1, replica_groups=mesh['samp'=8,'par'=4] {'samp'}, dimensions={0}, use_global_device_ids=true | all-gather | bytes 18432 | tf_op jit(solution)/shard_map/all_gather | solution.py:39
  156.9 34.2 %all-reduce.3.cloned.1.call-done = f32[512,512]{1,0:T(8,128)} async-done(((f32[512,512]{1,0:T(8,128)}), f32[512,512]{1,0:T(8,128)}) %all-reduce.3.cloned.1.call-update) | async-done | bytes 1048592 | tf_op jit(solution)/shard_map/psum | solution.py:34
  191.1 0.2 all-gather.4.cloned.1.call-start
  191.3 8.9 %fusion.1 = bf16[512,8192]{1,0:T(8,128)(2,1)} fusion(bf16[64,8,8192]{2,0,1:T(8,128)(2,1)} %copy-done, f32[8192]{0:T(1024)S(1)} %broadcast_multiply_fusion), kind=kLoop, calls=%fused_computation.4 | loop fusion | flops 16777216 | bytes 16809984 | tf_op jit(solution)/shard_map/convert_element_type | solution.py:32
  200.2 50.0 %all-reduce.5.cloned.1.call-done = f32[512,512]{1,0:T(8,128)} async-done(((f32[512,512]{1,0:T(8,128)}), f32[512,512]{1,0:T(8,128)}) %all-reduce.5.cloned.1.call-update) | async-done | bytes 1048592 | tf_op jit(solution)/shard_map/psum | solution.py:33
  250.2 1.6 copy.48
  251.9 0.7 gather_fusion
  252.7 0.6 gather_fusion.1
  253.3 0.3 convolution_add_fusion
  253.8 5.8 %cholesky.33 = f32[64,64]{1,0:T(8,128)S(1)} custom-call(f32[64,64]{1,0:T(8,128)S(1)} %fusion.29), custom_call_target="Cholesky" | custom-call | tf_op jit(solution)/shard_map/jit(cholesky)/cholesky | solution.py:44
  259.7 0.6 compare_reduce_fusion.3
  260.3 0.7 fusion.20
  261.0 4.9 %custom-call.24 = f32[1,64,64]{1,2,0:T(8,128)S(1)} custom-call(f32[1,64,64]{2,1,0:T(8,128)S(1)} %fusion.20), custom_call_target="InvertDiagBlocksLowerTriangular" | custom-call | tf_op jit(solution)/shard_map/triangular_solve/custom-call.3 | solution.py:13
  265.9 0.3 fusion.7
  266.5 0.3 convolution_subtract_fusion.2
  267.0 1.8 convolution_add_fusion.4
  269.0 0.7 cholesky.94
  269.8 0.6 compare_reduce_fusion.2
  270.4 0.6 fusion.44
  271.1 0.6 custom-call.26
  271.7 0.2 fusion.55
  272.0 0.2 convolution_subtract_fusion.1
  272.2 0.2 fusion.31
  272.5 0.7 cholesky.105
  273.2 0.6 compare_reduce_fusion.1
  273.9 0.6 fusion.45
  274.5 0.6 custom-call.30
  275.2 0.3 fusion.4
  275.8 0.3 fusion.2
  276.2 0.2 fusion.51
  276.5 0.2 convolution_add_fusion.3
  276.7 0.6 convolution_add_fusion.2
  277.5 0.7 cholesky.116
  278.3 0.6 compare_reduce_fusion
  279.0 0.6 fusion.46
  279.6 0.6 custom-call.32
  280.6 0.2 convolution_add_fusion.1
  280.8 5.2 %convolution_convert_fusion = bf16[8192,8]{0,1:T(8,128)(2,1)} fusion(bf16[512,8192]{1,0:T(8,128)(2,1)} %fusion.1, f32[512,8]{0,1:T(8,128)S(1)} %convolution_add_fusion.1), kind=kOutput, calls=%fused_computation.6 | convolution fusion | flops 67178496 | bytes 8536064 | tf_op jit(solution)/shard_map/rc,rv->cv/dot_general | solution.py:68
  286.1 0.7 constant_dynamic-slice_fusion
  286.7 22.1 %all-gather.4.cloned.1.call-done = bf16[65536,8]{0,1:T(8,128)(2,1)} async-done(((bf16[8192,8]{0,1:T(8,128)(2,1)}), bf16[65536,8]{0,1:T(8,128)(2,1)}) %all-gather.4.cloned.1.call-update) | async-done | bytes 1048592 | tf_op jit(solution)/shard_map/all_gather | solution.py:71
  308.8 2.7 convert_element_type.49
  (48 shorter events, 3.1 us)
Async XLA Ops:
  7.2 183.9 %all-reduce.3.cloned.1.call-start = ((), (), s32[]{:S(2)}) async-start(), calls=%async_computation.1 | async-start | bytes 2097152 | tf_op jit(solution)/shard_map/psum | solution.py:34
  114.0 3.2 %copy-start = (bf16[64,8,8192]{2,0,1:T(8,128)(2,1)}, bf16[64,8,8192]{2,0,1:T(8,128)(2,1)S(1)}, u32[]{:S(2)}) copy-start(bf16[64,8,8192]{2,0,1:T(8,128)(2,1)S(1)} %all_to_all.13) | copy-start | bytes 25165828
  128.3 11.4 %copy-start.3 = (s32[1,8]{1,0:T(1,128)S(1)}, s32[1,8]{1,0:T(1,128)}, u32[]{:S(2)}) copy-start(s32[1,8]{1,0:T(1,128)} %param.14) | copy-start | bytes 100
  128.3 19.5 %copy-start.2 = (f32[64,8]{0,1:T(8,128)S(1)}, f32[64,8]{0,1:T(8,128)}, u32[]{:S(2)}) copy-start(f32[64,8]{0,1:T(8,128)} %param.13) | copy-start | bytes 6148
  139.6 110.6 %all-reduce.5.cloned.1.call-start = ((), (), s32[]{:S(2)}) async-start(), calls=%async_computation.2 | async-start | bytes 2097152 | tf_op jit(solution)/shard_map/psum | solution.py:33
  191.1 117.8 %all-gather.4.cloned.1.call-start = ((), (), s32[]{:S(2)}) async-start(), calls=%async_computation.3 | async-start | bytes 1179648 | tf_op jit(solution)/shard_map/all_gather | solution.py:71
  250.2 26.5 %copy-start.1 = (f32[512,512]{1,0:T(8,128)S(1)}, f32[512,512]{1,0:T(8,128)}, u32[]{:S(2)}) copy-start(f32[512,512]{1,0:T(8,128)} %all-reduce.5.cloned.1.call-done) | copy-start | bytes 3145732
Sparse Core Ops, SparseCore 0:
  139.7 51.3 all-reduce.2
  194.2 55.9 all-reduce.4
  286.2 22.6 all-gather.3
